TPU v7x, 32 devices: a whole 2x2x4 slice. The times are simulated.
32 devices in a mesh: dp: 1, sp: 32 (over x, y, z, core).
Axes of the slice: x: 2, y: 2, z: 4, core: 2. Of those that a mesh axis runs over, the one named last changes fastest.
Arguments:
- q: bfloat16 [32, 64, 112], P('dp')
- k: bfloat16 [32, 4096, 64, 112], P('dp', 'sp')
- v: bfloat16 [32, 4096, 64, 112], P('dp', 'sp')
Outputs:
- q: bfloat16 [32, 64, 112], P('dp')
All inputs are finite; a program needn't handle non-finite values.
Results may differ from a plain program's by a relative error of at most 0.012.
Values are sent between devices in bfloat16 or wider.
A program may use at most 2 GiB of HBM per device.

v0:
```python
import jax
import jax.numpy as jnp
from jax import lax
from jax.sharding import PartitionSpec as P


def einsum(form, a, b):
    return jnp.einsum(form, a.astype(jnp.float32), b.astype(jnp.float32))


def part_of(q, k, v):
    grouped = q.reshape(q.shape[0], k.shape[2], -1, q.shape[2])
    scores = einsum("bgsd,bugd->bgsu", grouped, k) * q.shape[2] ** -0.5
    high = jnp.max(scores, -1, keepdims=True)
    weights = jnp.exp(scores - high)
    seen = einsum("bgsu,bugd->bgsd", weights.astype(jnp.bfloat16), v)
    return jnp.concatenate([seen, jnp.sum(weights, -1, keepdims=True), high], -1)


def together(parts):
    seen, total, high = parts[..., :-2], parts[..., -2:-1], parts[..., -1:]
    scale = jnp.exp(high - jnp.max(high, 0))
    return (jnp.sum(seen * scale, 0) / jnp.sum(total * scale, 0)).astype(jnp.bfloat16)


def solution(mesh):
    def step(q, k, v):
        return together(lax.all_gather(part_of(q, k, v), "sp")).reshape(q.shape)

    return jax.shard_map(
        step,
        mesh=mesh,
        in_specs=(P("dp", None, None), P("dp", "sp", None, None), P("dp", "sp", None, None)),
        out_specs=P("dp", None, None),
        check_vma=False,
    )
```

profile of v0, /device:TPU:0, one launch (start us, length us, event | category | flops | bytes accessed | tf_op | source)
XLA Modules:
  0.0 430.8 jit_solution(1632606429487639049)
XLA Ops:
  6.5 0.0 all-gather.3.cloned.1.call-start
  6.5 22.7 %fusion.3 = f32[32,64,1,128]{3,2,1,0:T(1,128)S(1)} fusion(bf16[32,128,64,112]{1,3,2,0:T(8,128)(2,1)} %param.4, bf16[32,64,112,1]{2,1,0,3:T(8,128)(2,1)} %bitcast.18), kind=kOutput, calls=%fused_computation.6 | convolution fusion | flops 58720256 | bytes 60227584 | tf_op jit(solution)/shard_map/bgsd,bugd->bgsu/dot_general | solution.py:8
  29.3 0.4 multiply_reduce_fusion
  29.6 0.7 fusion.7
  30.3 35.7 %fusion.1 = f32[32,64,1,112]{3,2,1,0:T(1,128)S(1)} fusion(bf16[32,128,64,112]{1,3,2,0:T(8,128)(2,1)} %param.5, bf16[32,64,128,1]{2,1,0,3:T(8,128)(2,1)S(1)} %get-tuple-element.7), kind=kOutput, calls=%fused_computation.4 | convolution fusion | flops 58720256 | bytes 60162048 | tf_op jit(solution)/shard_map/bgsu,bugd->bgsd/dot_general | solution.py:8
  66.0 1.1 copy.10
  67.1 1.5 pad_maximum_fusion
  68.6 0.0 all-gather.3.cloned.1.call-update
  68.6 332.1 %all-gather.3.cloned.1.call-done = f32[1024,64,1,114]{1,0,3,2:T(8,128)} async-done(((f32[32,64,1,114]{1,0,3,2:T(8,128)}), f32[1024,64,1,114]{1,0,3,2:T(8,128)}) %all-gather.3.cloned.1.call-update) | async-done | bytes 29884432 | tf_op jit(solution)/shard_map/all_gather | solution.py:28
  400.7 1.1 slice_reduce_fusion
  401.8 1.3 fusion.8
  403.1 18.9 %fusion = f32[32,64,112]{1,0,2:T(8,128)S(1)} fusion(f32[32,32,64,1,114]{2,1,0,4,3:T(8,128)} %bitcast.15, f32[32,32,64]{2,1,0:T(8,128)S(1)} %get-tuple-element.6), kind=kLoop, calls=%fused_computation.1 | loop fusion | flops 14450688 | bytes 30539776 | tf_op jit(solution)/shard_map/reduce_sum | solution.py:23
  422.0 0.2 divide_convert_fusion
  422.2 1.7 copy.6
Async XLA Ops:
  6.5 394.2 %all-gather.3.cloned.1.call-start = ((), (), s32[]{:S(2)}) async-start(), calls=%async_computation | async-start | bytes 61636608 | tf_op jit(solution)/shard_map/all_gather | solution.py:28
Sparse Core Ops, SparseCore 0:
  68.8 331.9 all-gather.2
where the time goes:
time: 431 us
  waiting for transfers between devices  332 us (77%)
  matrix products  58.5 us (14%)
  other arithmetic  24 us (6%)
  between operations  13.4 us (3%)
    all_gather x1, waiting for transfers between devices, step(): return together(lax.all_gather(part_of(q, k, v), 'sp')).reshape(q.shape)  332 us
    dot_general x2, matrix products, einsum(): return jnp.einsum(form, a.astype(jnp.float32), b.astype(jnp.float32))  58.5 us
    reduce_sum x1, other arithmetic, together(): jnp.sum(seen * scale, 0) / jnp.sum(total * scale, 0)  18.9 us
  transfers between devices with their start and end apart: 1, of which 1 were waited for; matrix products, arithmetic and copies ran while one was open for 0% of the time, Pallas kernels for 0%

commit v1 on v0

v1 whole, which is shorter than its diff:
```python
import functools

import jax
import jax.numpy as jnp
from jax import lax
from jax.experimental import pallas as pl
from jax.experimental.pallas import tpu as pltpu
from jax.sharding import PartitionSpec as P

F32 = jnp.float32
BF16 = jnp.bfloat16
DEPTH = 6
LAG = 5
PIECE = 16
OWNERS = 8


def owner_of(turn, piece):
    inner, upper = turn // 4, turn % 2
    return piece * 8 + (3 * upper + inner * (1 - 2 * upper)) * 2 + (turn % 4) // 2


def place_of(me):
    z = (me // 2) % 4
    return 4 * (((z + 1) // 2) % 2) + 2 * (me % 2) + z // 2, me // 8


def scores(q, keys, scale):
    row = lax.broadcasted_iota(jnp.int32, (8, 1), 0)
    tokens = keys(0).shape[1]
    left = right = jnp.zeros((8, tokens), F32)
    for i in range(8):
        got = jnp.dot(q, jnp.concatenate([keys(i), keys(8 + i)], 1), preferred_element_type=F32)
        left = jnp.where(row == i, got[:8, :tokens], left)
        right = jnp.where(row == i, got[8:, tokens:], right)
    score = jnp.concatenate([left, right], 0) * scale
    high = jnp.max(score, -1, keepdims=True)
    weight = jnp.exp(score - high)
    total = jnp.sum(weight, -1, keepdims=True)
    zero = jnp.zeros((8, tokens), F32)
    left = jnp.concatenate([weight[:8], zero], 1)
    right = jnp.concatenate([zero, weight[8:]], 1)
    return jnp.concatenate([left, right], 0).astype(BF16), total, high


def values(weight, vals):
    row = lax.broadcasted_iota(jnp.int32, (8, 1), 0)
    left = right = jnp.zeros((8, vals(0).shape[0]), F32)
    for i in range(8):
        both = jnp.concatenate([vals(i), vals(8 + i)], 1)
        got = lax.dot_general(weight, both, (((1,), (1,)), ((), ())), preferred_element_type=F32)
        left = jnp.where(row == i, got[:8], left)
        right = jnp.where(row == i, got[8:], right)
    return jnp.concatenate([left, right], 0)


def kernel(n, q_ref, k_hbm, v_hbm, o_ref, kbuf, vbuf, part, full, stat, rpart, rstat, ksem, vsem, psend, ssend, asend, precv, srecv, arecv):
    batch, heads, head = q_ref.shape
    pieces = heads // PIECE
    rounds = batch // OWNERS
    me = lax.axis_index("sp")
    my_turn, my_piece = place_of(me)
    scale = head**-0.5

    def fetch(t, slot):
        k = pltpu.make_async_copy(k_hbm.at[t], kbuf.at[slot], ksem.at[slot])
        v = pltpu.make_async_copy(v_hbm.at[t], vbuf.at[slot], vsem.at[slot])
        return k, v

    def remote(src, dst, send, recv, device):
        return pltpu.make_async_remote_copy(
            src_ref=src, dst_ref=dst, send_sem=send, recv_sem=recv, device_id={"sp": device}, device_id_type=pl.DeviceIdType.MESH
        )

    def drain(ref, sem):
        pltpu.make_async_copy(ref, ref, sem).wait()

    for t in range(DEPTH):
        for copy in fetch(t, t):
            copy.start()

    barrier = pltpu.get_barrier_semaphore()

    def greet(i, _):
        pl.semaphore_signal(barrier, inc=1, device_id={"sp": lax.rem(me + 1 + i, n)}, device_id_type=pl.DeviceIdType.MESH)
        return 0

    lax.fori_loop(0, n - 1, greet, 0)
    pl.semaphore_wait(barrier, n - 1)

    lane = lax.broadcasted_iota(jnp.int32, (PIECE, 128), 1)
    row = lax.broadcasted_iota(jnp.int32, (PIECE, 128), 0)

    def combine(turn):
        t = turn * OWNERS + my_turn
        rows = pl.ds(pl.multiple_of(my_piece * PIECE, PIECE), PIECE)
        drain(rpart.at[pl.ds(turn * n, n - 1)], precv.at[turn])
        drain(rstat.at[pl.ds(turn * n, n - 1)], srecv.at[turn])
        rpart[turn * n + me] = jnp.zeros((PIECE, head), BF16)
        own = stat[t]
        rstat[turn * n + me] = own
        got = rstat[pl.ds(turn * n, n)].reshape(n, 128)
        high = jnp.max(got, 0, keepdims=True)
        weight = jnp.exp(got - high)
        total = jnp.sum(pltpu.roll(got, 64, 1) * weight, 0, keepdims=True)
        share = weight / total
        mask = lane == my_piece * PIECE + row

        def column(line):
            return jnp.sum(jnp.where(mask, line, 0.0), -1, keepdims=True)

        acc = full[t, rows, :] * column(jnp.exp(own - high) / total)
        for src in range(n):
            acc += rpart[turn * n + src].astype(F32) * column(share[src : src + 1])
        o_ref[t, rows, :] = acc.astype(o_ref.dtype)

        def spread(i, _):
            piece = o_ref.at[t, rows]
            remote(piece, piece, asend, arecv, lax.rem(me + 1 + i, n)).start()
            return 0

        lax.fori_loop(0, n - 1, spread, 0)

    def step(t, _):
        slot = lax.rem(t, DEPTH)
        for copy in fetch(t, slot):
            copy.wait()
        got = [scores(q_ref[t, pl.ds(PIECE * c, PIECE), :], lambda i: kbuf[slot, PIECE * c + i], scale) for c in range(pieces)]
        line = jnp.zeros((PIECE, 128), F32)
        for c, (_, total, high) in enumerate(got):
            line = jnp.where(lane == PIECE * c + row, high, line)
            line = jnp.where(lane == heads + PIECE * c + row, total, line)
        stat[t] = jnp.sum(line, 0, keepdims=True)
        for c, (weight, _, _) in enumerate(got):
            out = values(weight, lambda i: vbuf[slot, PIECE * c + i])
            full[t, pl.ds(PIECE * c, PIECE), :] = out
            part[t, pl.ds(PIECE * c, PIECE), :] = out.astype(BF16)

        @pl.when(t + DEPTH < batch)
        def _():
            for copy in fetch(t + DEPTH, slot):
                copy.start()

        turn, place = t // OWNERS, lax.rem(t, OWNERS)
        for c in range(pieces):
            owner = owner_of(place, c)

            @pl.when(owner != me)
            def _():
                remote(part.at[t, pl.ds(PIECE * c, PIECE)], rpart.at[turn * n + me], psend, precv.at[turn], owner).start()
                remote(stat.at[t], rstat.at[turn * n + me], ssend, srecv.at[turn], owner).start()

        late = t - my_turn - LAG

        @pl.when((late >= 0) & (lax.rem(late + OWNERS, OWNERS) == 0))
        def _():
            combine(late // OWNERS)

        return 0

    lax.fori_loop(0, batch, step, 0)

    @pl.when(my_turn + LAG >= OWNERS)
    def _():
        combine(rounds - 1)

    drain(part.at[pl.ds(0, n - 1)], psend)
    drain(rstat.at[pl.ds(0, (n - 1) * rounds)], ssend)
    drain(o_ref.at[pl.ds(0, n - 1)], asend)
    drain(o_ref.at[pl.ds(0, n - 1)], arecv)


def solution(mesh):
    n = mesh.shape["sp"]

    def step(q, k, v):
        batch, tokens, heads, head = k.shape
        rounds, pieces = batch // OWNERS, heads // PIECE
        return pl.pallas_call(
            functools.partial(kernel, n),
            out_shape=jax.ShapeDtypeStruct(q.shape, q.dtype),
            in_specs=[pl.BlockSpec(memory_space=pltpu.VMEM), pl.BlockSpec(memory_space=pl.ANY), pl.BlockSpec(memory_space=pl.ANY)],
            out_specs=pl.BlockSpec(memory_space=pltpu.VMEM),
            scratch_shapes=[
                pltpu.VMEM((DEPTH, heads, head, tokens), k.dtype),
                pltpu.VMEM((DEPTH, heads, head, tokens), v.dtype),
                pltpu.VMEM((batch, heads, head), BF16),
                pltpu.VMEM((batch, heads, head), F32),
                pltpu.VMEM((batch, 1, 128), F32),
                pltpu.VMEM((rounds * n, PIECE, head), BF16),
                pltpu.VMEM((rounds * n, 1, 128), F32),
                pltpu.SemaphoreType.DMA((DEPTH,)),
                pltpu.SemaphoreType.DMA((DEPTH,)),
                pltpu.SemaphoreType.DMA,
                pltpu.SemaphoreType.DMA,
                pltpu.SemaphoreType.DMA,
                pltpu.SemaphoreType.DMA((rounds,)),
                pltpu.SemaphoreType.DMA((rounds,)),
                pltpu.SemaphoreType.DMA,
            ],
            compiler_params=pltpu.CompilerParams(vmem_limit_bytes=60 << 20, collective_id=0, has_side_effects=True),
        )(q, k.transpose(0, 2, 3, 1), v.transpose(0, 2, 3, 1))

    return jax.shard_map(
        step,
        mesh=mesh,
        in_specs=(P("dp", None, None), P("dp", "sp", None, None), P("dp", "sp", None, None)),
        out_specs=P("dp", None, None),
        check_vma=False,
    )
```

time: 431 us -> 52.1 us (0.12)
  waiting for transfers between devices: 332 us -> 0 us
  matrix products: 58.5 us -> 0 us
  Pallas kernels: 0 us -> 50.1 us
  other arithmetic: 24 us -> 0 us
  between operations: 13.4 us -> 0.01 us
    all_gather x1 -> x0, waiting for transfers between devices: 332 us -> none  [step(): return together(lax.all_gather(part_of(q, k, v), 'sp')).reshape(q.shape)]
    dot_general x2 -> x0, matrix products: 58.5 us -> none  [einsum(): return jnp.einsum(form, a.astype(jnp.float32), b.astype(jnp.float32))]
    pallas_call x0 -> x1, Pallas kernels: none -> 50.1 us  [step(): pl.pallas_call(functools.partial(kernel, n), out_shape=jax.ShapeDtypeStru...]
    reduce_sum x2 -> x0, other arithmetic: 20.2 us -> none  [the longest x1 18.9 us: together(): jnp.sum(seen * scale, 0) / jnp.sum(total * scale, 0)]
  transfers between devices with their start and end apart: 1 -> 0, of which waited for: 1 -> 0; matrix products, arithmetic and copies ran while one was open for 0% -> 0% of each run, Pallas kernels for 0% -> 0%
where the time goes in v1:
time: 52.1 us; the launch traced here: 51.9 us
  Pallas kernels  50.1 us (96%)
  local copies, waits for them, and re-layouts  1.87 us (4%)
    pallas_call x1, Pallas kernels, step(): pl.pallas_call(functools.partial(kernel, n), out_shape=jax.ShapeDtypeStru...  50.1 us
    unnamed x1, local copies, waits for them, and re-layouts  1.87 us

profile of v1, /device:TPU:0, one launch (start us, length us, event | category | flops | bytes accessed | tf_op | source)
XLA Modules:
  0.0 51.9 jit_solution(1946228388244639449)
XLA Ops:
  0.0 50.1 %shard_map.37 = bf16[32,64,112]{2,1,0:T(8,128)(2,1)} custom-call(bf16[32,64,112]{2,1,0:T(8,128)(2,1)} %q_ref.1, bf16[32,64,112,128]{3,2,1,0:T(8,128)(2,1)} %bitcast.2, bf16[32,64,112,128]{3,2,1,0:T(8,128)(2,1)} %bitcast.3), custom_call_target="tpu_custom_call" | custom-call | tf_op jit(solution)/shard_map/pallas_call | solution.py:179
  50.1 1.9 %copy.5 = bf16[32,64,112]{2,1,0:T(8,128)(2,1)} copy(bf16[32,64,112]{2,1,0:T(8,128)(2,1)} %shard_map.37) | data formatting | bytes 917504

commit v2 on v1

--- a/solution.py
+++ b/solution.py
@@ -9,20 +9,25 @@
 
 F32 = jnp.float32
 BF16 = jnp.bfloat16
-DEPTH = 6
-LAG = 5
+DEPTH = 5
+LAG = 7
 PIECE = 16
 OWNERS = 8
 
 
+def flip(z, piece):
+    return z + (piece % 2) * (3 - 2 * z)
+
+
 def owner_of(turn, piece):
     inner, upper = turn // 4, turn % 2
-    return piece * 8 + (3 * upper + inner * (1 - 2 * upper)) * 2 + (turn % 4) // 2
+    return piece * 8 + flip(3 * upper + inner * (1 - 2 * upper), piece) * 2 + (turn % 4) // 2
 
 
 def place_of(me):
-    z = (me // 2) % 4
-    return 4 * (((z + 1) // 2) % 2) + 2 * (me % 2) + z // 2, me // 8
+    piece = me // 8
+    z = flip((me // 2) % 4, piece)
+    return 4 * (((z + 1) // 2) % 2) + 2 * (me % 2) + z // 2, piece
 
 
 def scores(q, keys, scale):
@@ -54,8 +59,9 @@
     return jnp.concatenate([left, right], 0)
 
 
-def kernel(n, q_ref, k_hbm, v_hbm, o_ref, kbuf, vbuf, part, full, stat, rpart, rstat, ksem, vsem, psend, ssend, asend, precv, srecv, arecv):
+def kernel(n, q_hbm, k_hbm, v_hbm, o_ref, q_ref, kbuf, vbuf, part, full, stat, rpart, rstat, qsem, ksem, vsem, psend, ssend, asend, precv, srecv, arecv):
     batch, heads, head = q_ref.shape
+    queries = pltpu.make_async_copy(q_hbm, q_ref, qsem)
     pieces = heads // PIECE
     rounds = batch // OWNERS
     me = lax.axis_index("sp")
@@ -75,6 +81,7 @@
     def drain(ref, sem):
         pltpu.make_async_copy(ref, ref, sem).wait()
 
+    queries.start()
     for t in range(DEPTH):
         for copy in fetch(t, t):
             copy.start()
@@ -87,6 +94,7 @@
 
     lax.fori_loop(0, n - 1, greet, 0)
     pl.semaphore_wait(barrier, n - 1)
+    queries.wait()
 
     lane = lax.broadcasted_iota(jnp.int32, (PIECE, 128), 1)
     row = lax.broadcasted_iota(jnp.int32, (PIECE, 128), 0)
@@ -116,15 +124,35 @@
 
         def spread(i, _):
             piece = o_ref.at[t, rows]
-            remote(piece, piece, asend, arecv, lax.rem(me + 1 + i, n)).start()
+            remote(piece, piece, asend, arecv, i + (i >= me).astype(jnp.int32)).start()
             return 0
 
         lax.fori_loop(0, n - 1, spread, 0)
+
+    def post(t):
+        turn, place = t // OWNERS, lax.rem(t, OWNERS)
+
+        def send(c):
+            rows = pl.ds(pl.multiple_of(PIECE * c, PIECE), PIECE)
+            owner = owner_of(place, c)
+            remote(part.at[t, rows], rpart.at[turn * n + me], psend, precv.at[turn], owner).start()
+            remote(stat.at[t], rstat.at[turn * n + me], ssend, srecv.at[turn], owner).start()
+
+        @pl.when(place != my_turn)
+        def _():
+            for c in range(pieces):
+                send(c)
+
+        @pl.when(place == my_turn)
+        def _():
+            for c in range(1, pieces):
+                send((my_piece + c) % pieces)
 
     def step(t, _):
         slot = lax.rem(t, DEPTH)
-        for copy in fetch(t, slot):
-            copy.wait()
+        key, value = fetch(t, slot)
+        key.wait()
+        value.wait()
         got = [scores(q_ref[t, pl.ds(PIECE * c, PIECE), :], lambda i: kbuf[slot, PIECE * c + i], scale) for c in range(pieces)]
         line = jnp.zeros((PIECE, 128), F32)
         for c, (_, total, high) in enumerate(got):
@@ -141,14 +169,7 @@
             for copy in fetch(t + DEPTH, slot):
                 copy.start()
 
-        turn, place = t // OWNERS, lax.rem(t, OWNERS)
-        for c in range(pieces):
-            owner = owner_of(place, c)
-
-            @pl.when(owner != me)
-            def _():
-                remote(part.at[t, pl.ds(PIECE * c, PIECE)], rpart.at[turn * n + me], psend, precv.at[turn], owner).start()
-                remote(stat.at[t], rstat.at[turn * n + me], ssend, srecv.at[turn], owner).start()
+        post(t)
 
         late = t - my_turn - LAG
 
@@ -178,10 +199,11 @@
         rounds, pieces = batch // OWNERS, heads // PIECE
         return pl.pallas_call(
             functools.partial(kernel, n),
-            out_shape=jax.ShapeDtypeStruct(q.shape, q.dtype),
-            in_specs=[pl.BlockSpec(memory_space=pltpu.VMEM), pl.BlockSpec(memory_space=pl.ANY), pl.BlockSpec(memory_space=pl.ANY)],
+            out_shape=pltpu.VMEM(q.shape, q.dtype),
+            in_specs=[pl.BlockSpec(memory_space=pl.ANY)] * 3,
             out_specs=pl.BlockSpec(memory_space=pltpu.VMEM),
             scratch_shapes=[
+                pltpu.VMEM(q.shape, q.dtype),
                 pltpu.VMEM((DEPTH, heads, head, tokens), k.dtype),
                 pltpu.VMEM((DEPTH, heads, head, tokens), v.dtype),
                 pltpu.VMEM((batch, heads, head), BF16),
@@ -189,6 +211,7 @@
                 pltpu.VMEM((batch, 1, 128), F32),
                 pltpu.VMEM((rounds * n, PIECE, head), BF16),
                 pltpu.VMEM((rounds * n, 1, 128), F32),
+                pltpu.SemaphoreType.DMA,
                 pltpu.SemaphoreType.DMA((DEPTH,)),
                 pltpu.SemaphoreType.DMA((DEPTH,)),
                 pltpu.SemaphoreType.DMA,

time: 52.1 us -> 47.8 us (0.917)
  Pallas kernels: 50.1 us -> 46.9 us
  local copies, waits for them, and re-layouts: 1.87 us -> 0.8 us
    pallas_call x1, Pallas kernels: 50.1 us -> 46.9 us  [step(): pl.pallas_call(functools.partial(kernel, n), out_shape=pltpu.VMEM(q.shape...]
    unnamed x1, local copies, waits for them, and re-layouts: 1.87 us -> 0.8 us
where the time goes in v2:
time: 47.8 us; the launch traced here: 47.7 us
  Pallas kernels  46.9 us (98%)
  local copies, waits for them, and re-layouts  0.8 us (2%)
    pallas_call x1, Pallas kernels, step(): pl.pallas_call(functools.partial(kernel, n), out_shape=pltpu.VMEM(q.shape...  46.9 us

profile of v2, /device:TPU:0, one launch (start us, length us, event | category | flops | bytes accessed | tf_op | source)
XLA Modules:
  0.0 47.7 jit_solution(14035612156558304143)
XLA Ops:
  0.0 46.9 %shard_map.37 = bf16[32,64,112]{2,1,0:T(8,128)(2,1)S(1)} custom-call(bf16[32,64,112]{2,1,0:T(8,128)(2,1)} %q_hbm.1, bf16[32,64,112,128]{3,2,1,0:T(8,128)(2,1)} %bitcast.2, bf16[32,64,112,128]{3,2,1,0:T(8,128)(2,1)} %bitcast.3), custom_call_target="tpu_custom_call" | custom-call | tf_op jit(solution)/shard_map/pallas_call | solution.py:200
  46.9 0.8 %copy.5 = bf16[32,64,112]{2,1,0:T(8,128)(2,1)} copy(bf16[32,64,112]{2,1,0:T(8,128)(2,1)S(1)} %shard_map.37) | data formatting | bytes 917504

commit v3 on v2

--- a/solution.py
+++ b/solution.py
@@ -48,15 +48,24 @@
     return jnp.concatenate([left, right], 0).astype(BF16), total, high
 
 
-def values(weight, vals):
+def values(first, second, vals):
     row = lax.broadcasted_iota(jnp.int32, (8, 1), 0)
-    left = right = jnp.zeros((8, vals(0).shape[0]), F32)
-    for i in range(8):
-        both = jnp.concatenate([vals(i), vals(8 + i)], 1)
-        got = lax.dot_general(weight, both, (((1,), (1,)), ((), ())), preferred_element_type=F32)
-        left = jnp.where(row == i, got[:8], left)
-        right = jnp.where(row == i, got[8:], right)
-    return jnp.concatenate([left, right], 0)
+    lane = lax.broadcasted_iota(jnp.int32, (1, 16), 1) % 8
+    head = vals(0).shape[0]
+    left = right = jnp.zeros((8, head), F32)
+    turned = jnp.zeros((head, 16), F32)
+    contract = (((1,), (1,)), ((), ()))
+    for i in range(0, 8, 2):
+        for j in (i, i + 1):
+            both = jnp.concatenate([vals(j), vals(8 + j)], 1)
+            got = lax.dot_general(first, both, contract, preferred_element_type=F32)
+            left = jnp.where(row == j, got[:8], left)
+            right = jnp.where(row == j, got[8:], right)
+        for j in (i, i + 1):
+            both = jnp.concatenate([vals(16 + j), vals(24 + j)], 1)
+            got = lax.dot_general(both, second, contract, preferred_element_type=F32)
+            turned = jnp.where(lane == j, got, turned)
+    return jnp.concatenate([left, right], 0), turned.T
 
 
 def kernel(n, q_hbm, k_hbm, v_hbm, o_ref, q_ref, kbuf, vbuf, part, full, stat, rpart, rstat, qsem, ksem, vsem, psend, ssend, asend, precv, srecv, arecv):
@@ -124,7 +133,8 @@
 
         def spread(i, _):
             piece = o_ref.at[t, rows]
-            remote(piece, piece, asend, arecv, i + (i >= me).astype(jnp.int32)).start()
+            there = jnp.where(t == batch - 1, i + (i >= me).astype(jnp.int32), lax.rem(me + 1 + i, n))
+            remote(piece, piece, asend, arecv, there).start()
             return 0
 
         lax.fori_loop(0, n - 1, spread, 0)
@@ -140,7 +150,7 @@
 
         @pl.when(place != my_turn)
         def _():
-            for c in range(pieces):
+            for c in range(pieces - 1, -1, -1):
                 send(c)
 
         @pl.when(place == my_turn)
@@ -159,10 +169,12 @@
             line = jnp.where(lane == PIECE * c + row, high, line)
             line = jnp.where(lane == heads + PIECE * c + row, total, line)
         stat[t] = jnp.sum(line, 0, keepdims=True)
-        for c, (weight, _, _) in enumerate(got):
-            out = values(weight, lambda i: vbuf[slot, PIECE * c + i])
-            full[t, pl.ds(PIECE * c, PIECE), :] = out
-            part[t, pl.ds(PIECE * c, PIECE), :] = out.astype(BF16)
+        for c in range(0, pieces, 2):
+            outs = values(got[c][0], got[c + 1][0], lambda i: vbuf[slot, PIECE * c + i])
+            for d, out in enumerate(outs):
+                rows = pl.ds(PIECE * (c + d), PIECE)
+                full[t, rows, :] = out
+                part[t, rows, :] = out.astype(BF16)
 
         @pl.when(t + DEPTH < batch)
         def _():

time: 47.8 us -> 47.5 us (level)
  no operation moved by 1% of the time
where the time goes in v3:
time: 47.5 us; the launch traced here: 47.4 us
  Pallas kernels  46.6 us (98%)
  local copies, waits for them, and re-layouts  0.8 us (2%)
    pallas_call x1, Pallas kernels, step(): pl.pallas_call(functools.partial(kernel, n), out_shape=pltpu.VMEM(q.shape...  46.6 us

profile of v3, /device:TPU:0, one launch (start us, length us, event | category | flops | bytes accessed | tf_op | source)
XLA Modules:
  0.0 47.4 jit_solution(5969260697080941208)
XLA Ops:
  0.0 46.6 %shard_map.37 = bf16[32,64,112]{2,1,0:T(8,128)(2,1)S(1)} custom-call(bf16[32,64,112]{2,1,0:T(8,128)(2,1)} %q_hbm.1, bf16[32,64,112,128]{3,2,1,0:T(8,128)(2,1)} %bitcast.2, bf16[32,64,112,128]{3,2,1,0:T(8,128)(2,1)} %bitcast.3), custom_call_target="tpu_custom_call" | custom-call | tf_op jit(solution)/shard_map/pallas_call | solution.py:212
  46.6 0.8 %copy.5 = bf16[32,64,112]{2,1,0:T(8,128)(2,1)} copy(bf16[32,64,112]{2,1,0:T(8,128)(2,1)S(1)} %shard_map.37) | data formatting | bytes 917504

commit v4 on v3

--- a/solution.py
+++ b/solution.py
@@ -127,9 +127,10 @@
             return jnp.sum(jnp.where(mask, line, 0.0), -1, keepdims=True)
 
         acc = full[t, rows, :] * column(jnp.exp(own - high) / total)
+        sums = [acc, *[jnp.zeros((PIECE, head), F32)] * 3]
         for src in range(n):
-            acc += rpart[turn * n + src].astype(F32) * column(share[src : src + 1])
-        o_ref[t, rows, :] = acc.astype(o_ref.dtype)
+            sums[src % 4] += rpart[turn * n + src].astype(F32) * column(share[src : src + 1])
+        o_ref[t, rows, :] = ((sums[0] + sums[1]) + (sums[2] + sums[3])).astype(o_ref.dtype)
 
         def spread(i, _):
             piece = o_ref.at[t, rows]

time: 47.5 us -> 47.6 us (level)
  no operation moved by 1% of the time
where the time goes in v4:
time: 47.6 us; the launch traced here: 47.4 us
  Pallas kernels  46.6 us (98%)
  local copies, waits for them, and re-layouts  0.8 us (2%)
    pallas_call x1, Pallas kernels, step(): pl.pallas_call(functools.partial(kernel, n), out_shape=pltpu.VMEM(q.shape...  46.6 us

profile of v4, /device:TPU:0, one launch (start us, length us, event | category | flops | bytes accessed | tf_op | source)
XLA Modules:
  0.0 47.4 jit_solution(2707332993135660278)
XLA Ops:
  0.0 46.6 %shard_map.37 = bf16[32,64,112]{2,1,0:T(8,128)(2,1)S(1)} custom-call(bf16[32,64,112]{2,1,0:T(8,128)(2,1)} %q_hbm.1, bf16[32,64,112,128]{3,2,1,0:T(8,128)(2,1)} %bitcast.2, bf16[32,64,112,128]{3,2,1,0:T(8,128)(2,1)} %bitcast.3), custom_call_target="tpu_custom_call" | custom-call | tf_op jit(solution)/shard_map/pallas_call | solution.py:213
  46.6 0.8 %copy.5 = bf16[32,64,112]{2,1,0:T(8,128)(2,1)} copy(bf16[32,64,112]{2,1,0:T(8,128)(2,1)S(1)} %shard_map.37) | data formatting | bytes 917504
